TPU v7x, 32 devices: a whole 2x2x4 slice. The times are simulated.
32 devices in a mesh: row: 4 (over z), col: 8 (over y, x, core).
Axes of the slice: x: 2, y: 2, z: 4, core: 2. Of those that a mesh axis runs over, the one named last changes fastest.
Arguments:
- points: float32 [131072, 64], P(('row', 'col')), may hold values from -6 to 6
- factor: float32 [131072, 512], P(('row', 'col')), may hold values from -0.06 to 0.06
- pivots: int32 [2, 128], replicated, may hold values from 0 to 131071, as said below
Outputs:
- factor_new: float32 [131072, 256], P(('row', 'col'))
- gram_rows: float32 [256, 768], replicated
Inputs may be any that keep to these rules, and one draw needn't show every extreme that they name: All 256 pivots are different points.
All inputs are finite; a program needn't handle non-finite values.
Results may differ from a plain program's by a relative error of at most 0.00013.
Values sent between devices are 32-bit elements; how exact they have to be, the bound alone decides.
No kernel may reach another device: no remote copies, remote signals or barrier semaphores. Data moves between devices by JAX's collectives and lax.ppermute only.
A program may use at most 128 MiB of HBM per device.

v0:
```python
import jax
import jax.numpy as jnp
from jax import lax
from jax.sharding import PartitionSpec as P

highest = lax.Precision.HIGHEST
nugget = 0.1


def kernel_block(left, right):
    cross = jnp.dot(left, right.T, precision=highest)
    dist = jnp.sum(left * left, 1)[:, None] + jnp.sum(right * right, 1)[None, :] - 2.0 * cross
    return jnp.exp(-dist / left.shape[1])


def pivot_inverse(pivot_points, pivot_factor):
    size = pivot_points.shape[0]
    identity = jnp.eye(size, dtype=jnp.float32)
    outer = jnp.dot(pivot_factor, pivot_factor.T, precision=highest)
    shift = nugget + jnp.max(jnp.sum(jnp.abs(outer), 1))
    core = kernel_block(pivot_points, pivot_points) - outer + shift * identity
    lower = jnp.linalg.cholesky(core)
    return jax.scipy.linalg.solve_triangular(lower, identity, lower=True)


def new_columns(rows_points, rows_factor, pivot_points, pivot_factor, inverse):
    resid = kernel_block(rows_points, pivot_points) - jnp.dot(
        rows_factor, pivot_factor.T, precision=highest
    )
    return jnp.dot(resid, inverse.T, precision=highest)


def pick_rows(table, indices, offset, count):
    local = indices - offset
    inside = (local >= 0) & (local < count)
    taken = jnp.take(table, jnp.clip(local, 0, count - 1), axis=0)
    return jnp.where(inside[:, None], taken, jnp.zeros_like(taken))


def body(points, factor, pivots):
    count = points.shape[0]
    width = points.shape[1]
    size = pivots.shape[1]
    offset = (lax.axis_index("row") * lax.axis_size("col") + lax.axis_index("col")) * count
    current = factor
    made = []
    local_rows = pick_rows(jnp.concatenate([points, factor], 1), pivots.reshape(-1), offset, count)
    fetched = lax.psum(local_rows, ("row", "col"))
    all_points = fetched[:, :width]
    all_factor = fetched[:, width:]
    for section in range(pivots.shape[0]):
        pivot_points = all_points[section * size : (section + 1) * size]
        pivot_factor = all_factor[section * size : (section + 1) * size]
        inverse = pivot_inverse(pivot_points, pivot_factor)
        fresh = new_columns(points, current, pivot_points, pivot_factor, inverse)
        at_pivots = new_columns(all_points, all_factor, pivot_points, pivot_factor, inverse)
        all_factor = jnp.concatenate([all_factor, at_pivots], 1)
        made.append(fresh)
        current = jnp.concatenate([current, fresh], 1)
    factor_new = jnp.concatenate(made, 1)
    terms = jnp.dot(factor_new.T, current, precision=highest)
    total = lax.psum(terms, ("row", "col"))
    return (factor_new, total / count)


def solution(mesh):
    in_specs = (P(("row", "col"), None), P(("row", "col"), None), P())
    out_specs = (P(("row", "col"), None), P())
    return jax.shard_map(body, mesh=mesh, in_specs=in_specs, out_specs=out_specs, check_vma=False)
```

profile of v0, /device:TPU:0, one launch (start us, length us, event | category | flops | bytes accessed | tf_op | source)
XLA Modules:
  0.0 412.9 jit_solution(3661174679678323361)
XLA Ops:
  7.2 0.0 all-reduce.3.cloned.1.call-start
  7.2 0.7 compare_and_fusion
  7.9 0.7 and_bitcast_fusion
  8.6 1.8 copy.5
  10.4 10.1 %pad_maximum_fusion = f32[4096,576]{1,0:T(8,128)} fusion(f32[4096,512]{1,0:T(8,128)} %param.7, f32[4096,64]{1,0:T(8,128)S(1)} %copy.5), kind=kLoop, calls=%fused_computation.7 | loop fusion | flops 2359296 | bytes 18874368 | tf_op jit(solution)/shard_map/concatenate | solution.py:47
  20.6 5.3 %gather_fusion = f32[256,576]{1,0:T(8,128)S(1)} fusion(f32[4096,576]{1,0:T(8,128)} %pad_maximum_fusion, s32[1024]{0:T(1024)S(1)} %pad_clamp_fusion), kind=kCustom, calls=%fused_computation | custom fusion | bytes 1180672 | tf_op jit(solution)/shard_map/jit(_take)/gather | solution.py:36
  25.9 1.0 select_select_fusion
  26.9 0.3 all-reduce.5.cloned.1.call-start
  27.2 0.1 copy-done
  27.3 0.1 multiply_reduce_fusion
  27.4 131.9 %all-reduce.3.cloned.1.call-done = f32[256,576]{1,0:T(8,128)} async-done(((f32[256,576]{1,0:T(8,128)}), f32[256,576]{1,0:T(8,128)}) %all-reduce.3.cloned.1.call-update) | async-done | bytes 589840 | tf_op jit(solution)/shard_map/psum | solution.py:48
  159.4 1.6 abs_reduce_fusion.1
  161.0 0.6 reduce_max.18
  162.2 1.0 multiply_reduce_fusion.2
  163.2 1.2 fusion.35
  164.4 0.1 copy.7
  164.6 11.7 %cholesky.44 = f32[128,128]{1,0:T(8,128)S(1)} custom-call(f32[128,128]{1,0:T(8,128)S(1)} %fusion.53), custom_call_target="Cholesky" | custom-call | tf_op jit(solution)/shard_map/jit(cholesky)/cholesky | solution.py:22
  176.3 0.6 compare_reduce_fusion.1
  176.9 0.7 fusion.48
  177.6 9.8 %custom-call.6 = f32[1,128,128]{1,2,0:T(8,128)S(1)} custom-call(f32[1,128,128]{2,1,0:T(8,128)S(1)} %fusion.48), custom_call_target="InvertDiagBlocksLowerTriangular" | custom-call | tf_op jit(solution)/shard_map/jit(_solve_triangular)/triangular_solve | solution.py:23
  187.4 0.3 fusion.46
  187.7 1.0 multiply_reduce_fusion.1
  188.7 1.2 fusion.25
  190.0 0.7 convolution_subtract_fusion
  190.6 0.3 fusion.64
  190.9 0.2 slice.40
  191.1 0.5 abs_reduce_fusion
  191.6 0.6 reduce_max.19
  192.9 0.3 fusion.37
  193.2 0.1 copy.11
  193.3 12.2 %cholesky.55 = f32[128,128]{1,0:T(8,128)S(1)} custom-call(f32[128,128]{1,0:T(8,128)S(1)} %fusion.51), custom_call_target="Cholesky" | custom-call | tf_op jit(solution)/shard_map/jit(cholesky)/cholesky | solution.py:22
  205.5 0.6 compare_reduce_fusion
  206.2 0.7 fusion.49
  206.8 9.8 %custom-call.7 = f32[1,128,128]{1,2,0:T(8,128)S(1)} custom-call(f32[1,128,128]{2,1,0:T(8,128)S(1)} %fusion.49), custom_call_target="InvertDiagBlocksLowerTriangular" | custom-call | tf_op jit(solution)/shard_map/jit(_solve_triangular)/triangular_solve | solution.py:23
  216.6 0.3 fusion.44
  216.9 3.9 fusion.21
  220.8 9.4 %fusion.16 = f32[4096,128]{1,0:T(8,128)S(1)} fusion(f32[4096,128]{1,0:T(8,128)S(1)} %fusion.21, f32[4096,512]{1,0:T(8,128)} %param.7, f32[256,576]{1,0:T(8,128)S(1)} %copy-done.1), kind=kOutput, calls=%fused_computation.20 | convolution fusion | flops 3221749760 | bytes 12845056 | tf_op jit(solution)/shard_map/dot_general | solution.py:27
  230.2 2.0 fusion.63
  232.2 1.8 copy.8
  234.1 11.5 %fusion.6 = f32[4096,128]{1,0:T(8,128)S(1)} fusion(f32[4096,128]{1,0:T(8,128)} %copy.8, f32[4096,512]{1,0:T(8,128)} %param.7, f32[256,128]{1,0:T(8,128)S(1)} %fusion.64, f32[256,512]{1,0:T(8,128)} %copy-done.2), kind=kOutput, calls=%fused_computation.8 | convolution fusion | flops 4029235200 | bytes 13238272 | tf_op jit(solution)/shard_map/dot_general | solution.py:27
  245.6 4.9 %fusion.15 = f32[4096,128]{1,0:T(8,128)S(1)} fusion(f32[4096,128]{1,0:T(8,128)S(1)} %fusion.6, f32[4096,64]{0,1:T(8,128)S(1)} %copy-done, f32[128]{0:T(128)S(1)} %get-tuple-element.6, f32[4096]{0:T(1024)S(1)} %multiply_reduce_fusion, f32[256,576]{1,0:T(8,128)} %all-reduce.3.cloned.1.call-done), kind=kOutput, calls=%fused_computation.18 | convolution fusion | flops 405798912 | bytes 5325312 | tf_op jit(solution)/shard_map/dot_general | solution.py:11
  250.5 3.3 fusion.65
  253.8 2.9 copy.13
  256.7 18.0 %fusion = f32[256,768]{1,0:T(8,128)} fusion(f32[4096,128]{1,0:T(8,128)} %copy.13, f32[4096,128]{1,0:T(8,128)} %copy.8, f32[4096,512]{1,0:T(8,128)} %param.7, f32[4096,128]{0,1:T(8,128)} %fusion.65, f32[4096,128]{0,1:T(8,128)S(1)} %fusion.63), kind=kOutput, calls=%fused_computation.1 | convolution fusion | flops 9671016448 | bytes 17563648 | tf_op jit(solution)/shard_map/dot_general | solution.py:61
  274.8 3.9 pad_maximum_fusion.1
  278.7 5.6 %copy.14 = f32[4096,256]{1,0:T(8,128)} copy(f32[4096,256]{0,1:T(8,128)} %pad_maximum_fusion.1) | data formatting | bytes 8388608
  284.3 119.4 %all-reduce.5.cloned.1.call-done = f32[256,768]{1,0:T(8,128)} async-done(((f32[256,768]{1,0:T(8,128)}), f32[256,768]{1,0:T(8,128)}) %all-reduce.5.cloned.1.call-update) | async-done | bytes 786448 | tf_op jit(solution)/shard_map/psum | solution.py:62
  403.7 2.1 broadcast_multiply_fusion
  (13 shorter events, 0.2 us)
Async XLA Ops:
  7.2 152.2 %all-reduce.3.cloned.1.call-start = ((), (), s32[]{:S(2)}) async-start(), calls=%async_computation | async-start | bytes 1310720 | tf_op jit(solution)/shard_map/psum | solution.py:48
  25.8 1.5 copy-start
  26.9 376.9 %all-reduce.5.cloned.1.call-start = ((), (), s32[]{:S(2)}) async-start(), calls=%async_computation.1 | async-start | bytes 1572864 | tf_op jit(solution)/shard_map/psum | solution.py:62
  159.4 30.6 %copy-start.1 = (f32[256,576]{1,0:T(8,128)S(1)}, f32[256,576]{1,0:T(8,128)}, u32[]{:S(2)}) copy-start(f32[256,576]{1,0:T(8,128)} %all-reduce.3.cloned.1.call-done) | copy-start | bytes 1769476
  191.1 29.7 %copy-start.2 = (f32[256,512]{1,0:T(8,128)}, f32[256,512]{1,0:T(8,128)S(1)}, u32[]{:S(2)}) copy-start(f32[256,512]{1,0:T(8,128)S(1)} %slice.40) | copy-start | bytes 1572868
Sparse Core Ops, SparseCore 0:
  27.0 132.3 all-reduce.2
  274.9 128.8 all-reduce.4
where the time goes:
time: 417 us; the launch traced here: 413 us
  waiting for transfers between devices  251 us (60%)
  other arithmetic  68 us (16%)
  matrix products  59.3 us (14%)
  local copies, waits for them, and re-layouts  18 us (4%)
  between operations  15.8 us (4%)
    psum x1, waiting for transfers between devices, body(): fetched = lax.psum(local_rows, ('row', 'col'))  132 us
    psum x1, waiting for transfers between devices, body(): total = lax.psum(terms, ('row', 'col'))  119 us
    another operation x6, other arithmetic, pivot_inverse(): lower = jnp.linalg.cholesky(core)  25.2 us
    dot_general x3, matrix products, new_columns(): jnp.dot(rows_factor, pivot_factor.T, precision=highest)  21.6 us
    another operation x4, other arithmetic, pivot_inverse(): return jax.scipy.linalg.solve_triangular(lower, identity, lower=True)  20.9 us
    dot_general x1, matrix products, body(): terms = jnp.dot(factor_new.T, current, precision=highest)  18 us
    dot_general x5, matrix products, kernel_block(): cross = jnp.dot(left, right.T, precision=highest)  11.4 us
    concatenate x1, other arithmetic, body(): jnp.concatenate([points, factor], 1)  10.1 us
  transfers between devices with their start and end apart: 2, of which 2 were waited for; matrix products, arithmetic and copies ran while one was open for 2% of the time, Pallas kernels for 0%

commit v1 on v0

--- a/solution.py
+++ b/solution.py
@@ -59,7 +59,7 @@
         current = jnp.concatenate([current, fresh], 1)
     factor_new = jnp.concatenate(made, 1)
     terms = jnp.dot(factor_new.T, current, precision=highest)
-    total = lax.psum(terms, ("row", "col"))
+    total = lax.psum(lax.psum(terms, "col"), "row")
     return (factor_new, total / count)
 
 

time: 417 us -> 388 us (0.930)
  waiting for transfers between devices: 251 us -> 223 us
    psum x1 -> x2, waiting for transfers between devices: 119 us -> 90.8 us  [body(): total = lax.psum(lax.psum(terms, 'col'), 'row')]
  transfers between devices with their start and end apart: 2 -> 3, of which waited for: 2 -> 3; matrix products, arithmetic and copies ran while one was open for 2% -> 3% of each run, Pallas kernels for 0% -> 0%
where the time goes in v1:
time: 388 us; the launch traced here: 384 us
  waiting for transfers between devices  223 us (57%)
  other arithmetic  68 us (18%)
  matrix products  59.3 us (15%)
  local copies, waits for them, and re-layouts  18 us (5%)
  between operations  15.5 us (4%)
    psum x1, waiting for transfers between devices, body(): fetched = lax.psum(local_rows, ('row', 'col'))  132 us
    psum x2, waiting for transfers between devices, body(): total = lax.psum(lax.psum(terms, 'col'), 'row')  90.8 us
    another operation x6, other arithmetic, pivot_inverse(): lower = jnp.linalg.cholesky(core)  25.2 us
    dot_general x3, matrix products, new_columns(): jnp.dot(rows_factor, pivot_factor.T, precision=highest)  21.6 us
    another operation x4, other arithmetic, pivot_inverse(): return jax.scipy.linalg.solve_triangular(lower, identity, lower=True)  20.9 us
    dot_general x1, matrix products, body(): terms = jnp.dot(factor_new.T, current, precision=highest)  18 us
    dot_general x5, matrix products, kernel_block(): cross = jnp.dot(left, right.T, precision=highest)  11.4 us
    concatenate x1, other arithmetic, body(): jnp.concatenate([points, factor], 1)  10.1 us
  transfers between devices with their start and end apart: 3, of which 3 were waited for; matrix products, arithmetic and copies ran while one was open for 3% of the time, Pallas kernels for 0%

profile of v1, /device:TPU:0, one launch (start us, length us, event | category | flops | bytes accessed | tf_op | source)
XLA Modules:
  0.0 384.0 jit_solution(12459187002654492945)
XLA Ops:
  7.2 0.7 compare_and_fusion
  7.9 0.7 and_bitcast_fusion
  8.6 1.8 copy.5
  10.4 10.1 %pad_maximum_fusion = f32[4096,576]{1,0:T(8,128)} fusion(f32[4096,512]{1,0:T(8,128)} %param.7, f32[4096,64]{1,0:T(8,128)S(1)} %copy.5), kind=kLoop, calls=%fused_computation.7 | loop fusion | flops 2359296 | bytes 18874368 | tf_op jit(solution)/shard_map/concatenate | solution.py:47
  20.6 5.3 %gather_fusion = f32[256,576]{1,0:T(8,128)S(1)} fusion(f32[4096,576]{1,0:T(8,128)} %pad_maximum_fusion, s32[1024]{0:T(1024)S(1)} %pad_clamp_fusion), kind=kCustom, calls=%fused_computation | custom fusion | bytes 1180672 | tf_op jit(solution)/shard_map/jit(_take)/gather | solution.py:36
  25.9 1.0 select_select_fusion
  26.9 0.3 all-reduce.6.cloned.1.call-start
  27.2 0.1 copy-done
  27.3 0.1 multiply_reduce_fusion
  27.4 131.9 %all-reduce.4.cloned.1.call-done = f32[256,576]{1,0:T(8,128)} async-done(((f32[256,576]{1,0:T(8,128)}), f32[256,576]{1,0:T(8,128)}) %all-reduce.4.cloned.1.call-update) | async-done | bytes 589840 | tf_op jit(solution)/shard_map/psum | solution.py:48
  159.4 1.6 abs_reduce_fusion.1
  161.0 0.6 reduce_max.18
  162.2 1.0 multiply_reduce_fusion.2
  163.2 1.2 fusion.35
  164.4 0.1 copy.7
  164.6 11.7 %cholesky.44 = f32[128,128]{1,0:T(8,128)S(1)} custom-call(f32[128,128]{1,0:T(8,128)S(1)} %fusion.53), custom_call_target="Cholesky" | custom-call | tf_op jit(solution)/shard_map/jit(cholesky)/cholesky | solution.py:22
  176.3 0.6 compare_reduce_fusion.1
  176.9 0.7 fusion.48
  177.6 9.8 %custom-call.6 = f32[1,128,128]{1,2,0:T(8,128)S(1)} custom-call(f32[1,128,128]{2,1,0:T(8,128)S(1)} %fusion.48), custom_call_target="InvertDiagBlocksLowerTriangular" | custom-call | tf_op jit(solution)/shard_map/jit(_solve_triangular)/triangular_solve | solution.py:23
  187.4 0.3 fusion.46
  187.7 1.0 multiply_reduce_fusion.1
  188.7 1.2 fusion.25
  190.0 0.7 convolution_subtract_fusion
  190.6 0.3 fusion.64
  190.9 0.2 slice.40
  191.1 0.5 abs_reduce_fusion
  191.6 0.6 reduce_max.19
  192.9 0.3 fusion.37
  193.2 0.1 copy.11
  193.3 12.2 %cholesky.55 = f32[128,128]{1,0:T(8,128)S(1)} custom-call(f32[128,128]{1,0:T(8,128)S(1)} %fusion.51), custom_call_target="Cholesky" | custom-call | tf_op jit(solution)/shard_map/jit(cholesky)/cholesky | solution.py:22
  205.5 0.6 compare_reduce_fusion
  206.2 0.7 fusion.49
  206.8 9.8 %custom-call.7 = f32[1,128,128]{1,2,0:T(8,128)S(1)} custom-call(f32[1,128,128]{2,1,0:T(8,128)S(1)} %fusion.49), custom_call_target="InvertDiagBlocksLowerTriangular" | custom-call | tf_op jit(solution)/shard_map/jit(_solve_triangular)/triangular_solve | solution.py:23
  216.6 0.3 fusion.44
  216.9 3.9 %fusion.21 = f32[4096,128]{1,0:T(8,128)S(1)} fusion(f32[4096,64]{0,1:T(8,128)S(1)} %copy-done, f32[128]{0:T(128)S(1)} %get-tuple-element.7, f32[4096]{0:T(1024)S(1)} %multiply_reduce_fusion, f32[256,576]{1,0:T(8,128)S(1)} %copy-done.1), kind=kOutput, calls=%fused_computation.26 | convolution fusion | flops 405274624 | bytes 3228160 | tf_op jit(solution)/shard_map/dot_general | solution.py:11
  220.8 9.4 %fusion.16 = f32[4096,128]{1,0:T(8,128)S(1)} fusion(f32[4096,128]{1,0:T(8,128)S(1)} %fusion.21, f32[4096,512]{1,0:T(8,128)} %param.7, f32[256,576]{1,0:T(8,128)S(1)} %copy-done.1), kind=kOutput, calls=%fused_computation.20 | convolution fusion | flops 3221749760 | bytes 12845056 | tf_op jit(solution)/shard_map/dot_general | solution.py:27
  230.2 2.0 fusion.63
  232.2 1.8 copy.8
  234.1 11.5 %fusion.6 = f32[4096,128]{1,0:T(8,128)S(1)} fusion(f32[4096,128]{1,0:T(8,128)} %copy.8, f32[4096,512]{1,0:T(8,128)} %param.7, f32[256,128]{1,0:T(8,128)S(1)} %fusion.64, f32[256,512]{1,0:T(8,128)} %copy-done.2), kind=kOutput, calls=%fused_computation.8 | convolution fusion | flops 4029235200 | bytes 13238272 | tf_op jit(solution)/shard_map/dot_general | solution.py:27
  245.6 4.9 %fusion.15 = f32[4096,128]{1,0:T(8,128)S(1)} fusion(f32[4096,128]{1,0:T(8,128)S(1)} %fusion.6, f32[4096,64]{0,1:T(8,128)S(1)} %copy-done, f32[128]{0:T(128)S(1)} %get-tuple-element.6, f32[4096]{0:T(1024)S(1)} %multiply_reduce_fusion, f32[256,576]{1,0:T(8,128)} %all-reduce.4.cloned.1.call-done), kind=kOutput, calls=%fused_computation.18 | convolution fusion | flops 405798912 | bytes 5325312 | tf_op jit(solution)/shard_map/dot_general | solution.py:11
  250.5 3.3 fusion.65
  253.8 2.9 copy.13
  256.7 18.0 %fusion = f32[256,768]{1,0:T(8,128)} fusion(f32[4096,128]{1,0:T(8,128)} %copy.13, f32[4096,128]{1,0:T(8,128)} %copy.8, f32[4096,512]{1,0:T(8,128)} %param.7, f32[4096,128]{0,1:T(8,128)} %fusion.65, f32[4096,128]{0,1:T(8,128)S(1)} %fusion.63), kind=kOutput, calls=%fused_computation.1 | convolution fusion | flops 9671016448 | bytes 17563648 | tf_op jit(solution)/shard_map/dot_general | solution.py:61
  274.8 54.8 %all-reduce.6.cloned.1.call-done = f32[256,768]{1,0:T(8,128)} async-done(((f32[256,768]{1,0:T(8,128)}), f32[256,768]{1,0:T(8,128)}) %all-reduce.6.cloned.1.call-update) | async-done | bytes 786448 | tf_op jit(solution)/shard_map/psum | solution.py:62
  329.6 3.9 %pad_maximum_fusion.1 = f32[4096,256]{0,1:T(8,128)} fusion(f32[4096,128]{0,1:T(8,128)} %fusion.65, f32[4096,128]{0,1:T(8,128)S(1)} %fusion.63), kind=kLoop, calls=%fused_computation.27 | loop fusion | flops 1048576 | bytes 8388608 | tf_op jit(solution)/shard_map/concatenate | solution.py:60
  333.5 5.6 %copy.14 = f32[4096,256]{1,0:T(8,128)} copy(f32[4096,256]{0,1:T(8,128)} %pad_maximum_fusion.1) | data formatting | bytes 8388608
  339.1 36.0 %all-reduce.8.cloned.1.call-done = f32[256,768]{1,0:T(8,128)} async-done(((f32[256,768]{1,0:T(8,128)}), f32[256,768]{1,0:T(8,128)}) %all-reduce.8.cloned.1.call-update) | async-done | bytes 786448 | tf_op jit(solution)/shard_map/psum | solution.py:62
  375.2 2.1 broadcast_multiply_fusion
  (16 shorter events, 0.3 us)
Async XLA Ops:
  7.2 152.2 %all-reduce.4.cloned.1.call-start = ((), (), s32[]{:S(2)}) async-start(), calls=%async_computation | async-start | bytes 1310720 | tf_op jit(solution)/shard_map/psum | solution.py:48
  25.8 1.5 copy-start
  26.9 302.7 %all-reduce.6.cloned.1.call-start = ((), (), s32[]{:S(2)}) async-start(), calls=%async_computation.1 | async-start | bytes 1572864 | tf_op jit(solution)/shard_map/psum | solution.py:62
  159.4 30.6 %copy-start.1 = (f32[256,576]{1,0:T(8,128)S(1)}, f32[256,576]{1,0:T(8,128)}, u32[]{:S(2)}) copy-start(f32[256,576]{1,0:T(8,128)} %all-reduce.4.cloned.1.call-done) | copy-start | bytes 1769476
  191.1 29.7 %copy-start.2 = (f32[256,512]{1,0:T(8,128)}, f32[256,512]{1,0:T(8,128)S(1)}, u32[]{:S(2)}) copy-start(f32[256,512]{1,0:T(8,128)S(1)} %slice.40) | copy-start | bytes 1572868
  274.8 100.4 %all-reduce.8.cloned.1.call-start = ((), (), s32[]{:S(2)}) async-start(), calls=%async_computation.2 | async-start | bytes 1572864 | tf_op jit(solution)/shard_map/psum | solution.py:62
Sparse Core Ops, SparseCore 0:
  27.0 132.3 all-reduce.3
  274.9 54.6 all-reduce.5
  332.0 43.1 all-reduce.7
